TPU v7x, 32 devices: a whole 2x2x4 slice. The times are simulated.
32 devices in a mesh: ctx: 4 (over z), kvh: 4 (over y, x), conv: 2 (over core).
Axes of the slice: x: 2, y: 2, z: 4, core: 2. Of those that a mesh axis runs over, the one named last changes fastest.
Arguments:
- queries: bfloat16 [2, 512, 64, 128], P('conv', 'ctx', 'kvh'), may hold values from -6 to 6
- keys: bfloat16 [2, 4096, 8, 128], P('conv', 'ctx', 'kvh'), may hold values from -6 to 6
- values: bfloat16 [2, 4096, 8, 128], P('conv', 'ctx', 'kvh'), may hold values from -6 to 6
- lengths: int32 [2], P('conv'), may hold values from 64 to 3584
Outputs:
- attended: bfloat16 [2, 512, 64, 128], P('conv', 'ctx', 'kvh')
Inputs may be any that keep to these rules, and one draw needn't show every extreme that they name: The new turn's keys and values stand at cache positions lengths to lengths + 511; later positions hold unused entries.
All inputs are finite; a program needn't handle non-finite values.
Results may differ from a plain program's by a relative error of at most 0.005.
Values may be sent and summed in bfloat16 or wider, within the bound.
No kernel may reach another device: no remote copies, remote signals or barrier semaphores. Data moves between devices by JAX's collectives and lax.ppermute only.
A program may use at most 64 MiB of HBM per device.

v0:
```python
import jax
import jax.numpy as jnp
from jax import lax
from jax.sharding import PartitionSpec as P

mask_fill = -1e30


def shards(queries, keys, values, lengths):
    conv_dev, tok_dev, head_dev, head_dim = queries.shape
    ctx_dev = keys.shape[1]
    kv_dev = keys.shape[2]
    group_size = head_dev // kv_dev
    cycle_size = lax.axis_size("ctx")
    score_scale = 1.0 / head_dim**0.5
    key_position = lax.axis_index("ctx") * ctx_dev + jnp.arange(ctx_dev, dtype=jnp.int32)
    piece_rows = lax.all_gather(queries, "ctx", axis=1, tiled=True)
    row_count = piece_rows.shape[1]
    block_size = 64
    block_total = row_count // block_size
    blocks = jnp.moveaxis(
        piece_rows.reshape(conv_dev, block_total, block_size, head_dev, head_dim), 1, 0
    )

    def one_block(block_args):
        query_block, block_index = block_args
        query_block = query_block.reshape(conv_dev, block_size, kv_dev, group_size, head_dim)
        scores = (
            jnp.einsum("cbkgd,cskd->ckbgs", query_block, keys, preferred_element_type=jnp.float32)
            * score_scale
        )
        query_position = (
            lengths[:, None]
            + block_index * block_size
            + jnp.arange(block_size, dtype=jnp.int32)[None, :]
        )
        visible = key_position[None, None, None, None, :] <= query_position[:, None, :, None, None]
        masked = jnp.where(visible, scores, mask_fill)
        row_max = jnp.max(masked, axis=-1)
        weights = jnp.where(visible, jnp.exp(masked - row_max[..., None]), 0.0)
        exp_total = jnp.sum(weights, axis=-1)
        rounded = weights.astype(jnp.bfloat16)
        weighted = jnp.einsum(
            "ckbgs,cskd->ckbgd", rounded, values, preferred_element_type=jnp.float32
        )
        safe_total = jnp.maximum(exp_total, 1.0)
        partial_value = (weighted / safe_total[..., None]).astype(jnp.bfloat16)
        log_total = row_max + jnp.log(safe_total)
        partial_value = jnp.transpose(partial_value, (0, 2, 1, 3, 4)).reshape(
            conv_dev, block_size, head_dev, head_dim
        )
        log_total = jnp.transpose(log_total, (0, 2, 1, 3)).reshape(conv_dev, block_size, head_dev)
        return (partial_value, log_total)

    partial_value, log_total = lax.map(
        one_block, (blocks, jnp.arange(block_total, dtype=jnp.int32))
    )
    partial_value = jnp.moveaxis(partial_value, 0, 1).reshape(
        conv_dev, row_count, head_dev, head_dim
    )
    log_total = jnp.moveaxis(log_total, 0, 1).reshape(conv_dev, row_count, head_dev)
    partial_value, log_total = (partial_value, log_total)
    arrived = lax.all_to_all(
        partial_value.reshape(conv_dev, cycle_size, tok_dev, head_dev, head_dim),
        "ctx",
        split_axis=1,
        concat_axis=1,
        tiled=True,
    )
    arrived_totals = lax.all_to_all(
        log_total.reshape(conv_dev, cycle_size, tok_dev, head_dev),
        "ctx",
        split_axis=1,
        concat_axis=1,
        tiled=True,
    )
    top = jnp.max(arrived_totals, axis=1)
    share = jnp.exp(arrived_totals - top[:, None])
    numerator = jnp.sum(share[..., None] * arrived.astype(jnp.float32), axis=1)
    denominator = jnp.sum(share, axis=1)
    return (numerator / denominator[..., None]).astype(jnp.bfloat16)


def solution(mesh):
    in_specs = (
        P("conv", "ctx", "kvh", None),
        P("conv", "ctx", "kvh", None),
        P("conv", "ctx", "kvh", None),
        P("conv"),
    )
    out_specs = P("conv", "ctx", "kvh", None)
    return jax.shard_map(shards, mesh=mesh, in_specs=in_specs, out_specs=out_specs, check_vma=False)
```

profile of v0, /device:TPU:0, one launch (start us, length us, event | category | flops | bytes accessed | tf_op | source)
XLA Modules:
  0.0 183.0 jit_solution(16355917170916339926)
XLA Ops:
  7.3 1.1 copy.20
  9.5 47.8 %all-gather.2.cloned.1.call-done = bf16[1,512,16,128]{3,2,0,1:T(8,128)(2,1)} async-done(((bf16[1,128,16,128]{3,2,0,1:T(8,128)(2,1)}), bf16[1,512,16,128]{3,2,0,1:T(8,128)(2,1)}) %all-gather.2.cloned.1.call-update) | async-done | bytes 2097168 | tf_op jit(solution)/shard_map/all_gather | solution.py:17
  57.3 57.1 %while.13 = (s32[]{:T(128)}, bf16[8,1,64,16,128]{4,3,2,1,0:T(8,128)(2,1)S(1)}, f32[8,1,64,16]{2,0,3,1:T(8,128)S(1)}, s32[8]{0:T(128)S(1)}, s32[1]{0:T(128)}, /*i...) while((s32[]{:T(128)}, ...), condition=%wide.region_3.4_spmd.clone, body=%wide.region_0.3_spmd.clone.sunk | while | flops 550831168 | bytes 15004841 | solution.py:55
  59.3 2.1 %fusion.34 = (f32[2,64,8]{2,1,0:T(8,128)S(1)}, f32[2,64,8,1024]{3,2,1,0:T(8,128)S(1)}) fusion(pred[64,1024]{1,0:T(8,128)(4,1)S(1)} %broadcast_compare_fusion.2, bf16[1,1024,2,128]{3,1,2,0:T(8,128)(2,1)S(1)} %get-tuple-element.220, bf16[8,1,64,16,128]{4,3,2,1,0:T(8,128)(2,1)} %get-tuple-element.219, s32[]{:T(128)} %get-tuple-element.202), kind=kOutput, calls=%fused_computation.3.clone.1 | convolution fusion | flops 271580160 | bytes 5050880 | tf_op jit(solution)/shard_map/while/body/eval_jaxpr/cbkgd,cskd->ckbgs/dot_general | solution.py:29
  61.4 1.5 fusion.35
  62.9 1.3 fusion.36
  66.5 2.1 %fusion.34 = (f32[2,64,8]{2,1,0:T(8,128)S(1)}, f32[2,64,8,1024]{3,2,1,0:T(8,128)S(1)}) fusion(pred[64,1024]{1,0:T(8,128)(4,1)S(1)} %broadcast_compare_fusion.2, bf16[1,1024,2,128]{3,1,2,0:T(8,128)(2,1)S(1)} %get-tuple-element.220, bf16[8,1,64,16,128]{4,3,2,1,0:T(8,128)(2,1)} %get-tuple-element.219, s32[]{:T(128)} %get-tuple-element.202), kind=kOutput, calls=%fused_computation.3.clone.1 | convolution fusion | flops 271580160 | bytes 5050880 | tf_op jit(solution)/shard_map/while/body/eval_jaxpr/cbkgd,cskd->ckbgs/dot_general | solution.py:29
  68.6 1.5 fusion.35
  70.1 1.3 fusion.36
  73.6 2.1 %fusion.34 = (f32[2,64,8]{2,1,0:T(8,128)S(1)}, f32[2,64,8,1024]{3,2,1,0:T(8,128)S(1)}) fusion(pred[64,1024]{1,0:T(8,128)(4,1)S(1)} %broadcast_compare_fusion.2, bf16[1,1024,2,128]{3,1,2,0:T(8,128)(2,1)S(1)} %get-tuple-element.220, bf16[8,1,64,16,128]{4,3,2,1,0:T(8,128)(2,1)} %get-tuple-element.219, s32[]{:T(128)} %get-tuple-element.202), kind=kOutput, calls=%fused_computation.3.clone.1 | convolution fusion | flops 271580160 | bytes 5050880 | tf_op jit(solution)/shard_map/while/body/eval_jaxpr/cbkgd,cskd->ckbgs/dot_general | solution.py:29
  75.7 1.5 fusion.35
  77.2 1.3 fusion.36
  80.8 2.1 %fusion.34 = (f32[2,64,8]{2,1,0:T(8,128)S(1)}, f32[2,64,8,1024]{3,2,1,0:T(8,128)S(1)}) fusion(pred[64,1024]{1,0:T(8,128)(4,1)S(1)} %broadcast_compare_fusion.2, bf16[1,1024,2,128]{3,1,2,0:T(8,128)(2,1)S(1)} %get-tuple-element.220, bf16[8,1,64,16,128]{4,3,2,1,0:T(8,128)(2,1)} %get-tuple-element.219, s32[]{:T(128)} %get-tuple-element.202), kind=kOutput, calls=%fused_computation.3.clone.1 | convolution fusion | flops 271580160 | bytes 5050880 | tf_op jit(solution)/shard_map/while/body/eval_jaxpr/cbkgd,cskd->ckbgs/dot_general | solution.py:29
  82.9 1.5 fusion.35
  84.4 1.3 fusion.36
  87.9 2.1 %fusion.34 = (f32[2,64,8]{2,1,0:T(8,128)S(1)}, f32[2,64,8,1024]{3,2,1,0:T(8,128)S(1)}) fusion(pred[64,1024]{1,0:T(8,128)(4,1)S(1)} %broadcast_compare_fusion.2, bf16[1,1024,2,128]{3,1,2,0:T(8,128)(2,1)S(1)} %get-tuple-element.220, bf16[8,1,64,16,128]{4,3,2,1,0:T(8,128)(2,1)} %get-tuple-element.219, s32[]{:T(128)} %get-tuple-element.202), kind=kOutput, calls=%fused_computation.3.clone.1 | convolution fusion | flops 271580160 | bytes 5050880 | tf_op jit(solution)/shard_map/while/body/eval_jaxpr/cbkgd,cskd->ckbgs/dot_general | solution.py:29
  90.0 1.5 fusion.35
  91.5 1.3 fusion.36
  95.0 2.1 %fusion.34 = (f32[2,64,8]{2,1,0:T(8,128)S(1)}, f32[2,64,8,1024]{3,2,1,0:T(8,128)S(1)}) fusion(pred[64,1024]{1,0:T(8,128)(4,1)S(1)} %broadcast_compare_fusion.2, bf16[1,1024,2,128]{3,1,2,0:T(8,128)(2,1)S(1)} %get-tuple-element.220, bf16[8,1,64,16,128]{4,3,2,1,0:T(8,128)(2,1)} %get-tuple-element.219, s32[]{:T(128)} %get-tuple-element.202), kind=kOutput, calls=%fused_computation.3.clone.1 | convolution fusion | flops 271580160 | bytes 5050880 | tf_op jit(solution)/shard_map/while/body/eval_jaxpr/cbkgd,cskd->ckbgs/dot_general | solution.py:29
  97.1 1.5 fusion.35
  98.6 1.3 fusion.36
  102.2 2.1 %fusion.34 = (f32[2,64,8]{2,1,0:T(8,128)S(1)}, f32[2,64,8,1024]{3,2,1,0:T(8,128)S(1)}) fusion(pred[64,1024]{1,0:T(8,128)(4,1)S(1)} %broadcast_compare_fusion.2, bf16[1,1024,2,128]{3,1,2,0:T(8,128)(2,1)S(1)} %get-tuple-element.220, bf16[8,1,64,16,128]{4,3,2,1,0:T(8,128)(2,1)} %get-tuple-element.219, s32[]{:T(128)} %get-tuple-element.202), kind=kOutput, calls=%fused_computation.3.clone.1 | convolution fusion | flops 271580160 | bytes 5050880 | tf_op jit(solution)/shard_map/while/body/eval_jaxpr/cbkgd,cskd->ckbgs/dot_general | solution.py:29
  104.3 1.5 fusion.35
  105.8 1.3 fusion.36
  109.3 2.1 %fusion.34 = (f32[2,64,8]{2,1,0:T(8,128)S(1)}, f32[2,64,8,1024]{3,2,1,0:T(8,128)S(1)}) fusion(pred[64,1024]{1,0:T(8,128)(4,1)S(1)} %broadcast_compare_fusion.2, bf16[1,1024,2,128]{3,1,2,0:T(8,128)(2,1)S(1)} %get-tuple-element.220, bf16[8,1,64,16,128]{4,3,2,1,0:T(8,128)(2,1)} %get-tuple-element.219, s32[]{:T(128)} %get-tuple-element.202), kind=kOutput, calls=%fused_computation.3.clone.1 | convolution fusion | flops 271580160 | bytes 5050880 | tf_op jit(solution)/shard_map/while/body/eval_jaxpr/cbkgd,cskd->ckbgs/dot_general | solution.py:29
  111.4 1.5 fusion.35
  112.9 1.3 fusion.36
  114.6 8.1 %all_to_all.10 = f32[1,4,128,16]{2,3,0,1:T(8,128)S(1)} all-to-all(f32[1,4,128,16]{2,3,0,1:T(8,128)S(1)} %copy.23), channel_id=1, replica_groups=mesh['ctx'=4,'kvh'=4,'conv'=2] {'ctx'}, dimensions={1} | all-to-all | bytes 65536 | tf_op jit(solution)/shard_map/all_to_all | solution.py:70
  122.7 3.6 %all-to-all-start.1 = ((bf16[1,4,128,16,128]{4,3,2,0,1:T(8,128)(2,1)}), bf16[1,4,128,16,128]{4,3,2,0,1:T(8,128)(2,1)S(1)}, u32[]{:S(2)}, u32[]{:S(2)}) async-start(bf16[1,4,128,16,128]{4,3,2,0,1:T(8,128)(2,1)} %bitcast.63), calls=%async_computation.1 | async-start | bytes 4194304 | tf_op jit(solution)/shard_map/all_to_all | solution.py:63
  126.6 46.9 %all-to-all-done.1 = bf16[1,4,128,16,128]{4,3,2,0,1:T(8,128)(2,1)S(1)} async-done(((bf16[1,4,128,16,128]{4,3,2,0,1:T(8,128)(2,1)}), bf16[1,4,128,16,128]{4,3,2,0,1:T(8,128)(2,1)S(1)}, u32[]{:S(2)}, u32[]{:S(2)}) %all-to-all-start.1) | async-done | bytes 2097184 | tf_op jit(solution)/shard_map/all_to_all | solution.py:63
  173.5 1.5 multiply_reduce_fusion
  175.0 1.1 fusion.24
  (78 shorter events, 9.6 us)
Async XLA Ops:
  6.5 50.8 %all-gather.2.cloned.1.call-start = ((), (), s32[]{:S(2)}) async-start(), calls=%async_computation.2 | async-start | bytes 2621440 | tf_op jit(solution)/shard_map/all_gather | solution.py:17
  114.5 8.2 %copy-start = (bf16[8,1,64,16,128]{4,3,2,1,0:T(8,128)(2,1)}, bf16[8,1,64,16,128]{4,3,2,1,0:T(8,128)(2,1)S(1)}, u32[]{:S(2)}) copy-start(bf16[8,1,64,16,128]{4,3,2,1,0:T(8,128)(2,1)S(1)} %get-tuple-element.54) | copy-start | bytes 6291460
  122.7 50.8 %all-to-all-start.1 = ((bf16[1,4,128,16,128]{4,3,2,0,1:T(8,128)(2,1)}), bf16[1,4,128,16,128]{4,3,2,0,1:T(8,128)(2,1)S(1)}, u32[]{:S(2)}, u32[]{:S(2)}) async-start(bf16[1,4,128,16,128]{4,3,2,0,1:T(8,128)(2,1)} %bitcast.63), calls=%async_computation.1 | async-start | bytes 4194304 | tf_op jit(solution)/shard_map/all_to_all | solution.py:63
Sparse Core Ops, SparseCore 0:
  8.9 48.3 all-gather.1
where the time goes:
time: 184 us; the launch traced here: 183 us
  waiting for transfers between devices  95.4 us (52%)
  matrix products  27.3 us (15%)
  other arithmetic  15.6 us (8%)
  between operations  13.5 us (7%)
  loops' own time  10.6 us (6%)
  local copies, waits for them, and re-layouts  8.89 us (5%)
  blocking collectives  8.11 us (4%)
  starting transfers between devices  3.61 us (2%)
    all_gather x1, waiting for transfers between devices, shards(): piece_rows = lax.all_gather(queries, 'ctx', axis=1, tiled=True)  47.8 us
    all_to_all x1, waiting for transfers between devices, shards(): lax.all_to_all(partial_value.reshape(conv_dev, cycle_size, tok_dev, head_...  46.9 us
    dot_general x8, matrix products, one_block(): jnp.einsum('cbkgd,cskd->ckbgs', query_block, keys, preferred_element_type...  16.8 us
    reduce_sum x8, other arithmetic, one_block(): exp_total = jnp.sum(weights, axis=-1)  11.8 us
    another operation x1, loops' own time, shards(): lax.map(one_block, (blocks, jnp.arange(block_total, dtype=jnp.int32)))  10.6 us
    dot_general x8, matrix products, one_block(): jnp.einsum('ckbgs,cskd->ckbgd', rounded, values, preferred_element_type=j...  10.5 us
    all_to_all x1, blocking collectives, shards(): lax.all_to_all(log_total.reshape(conv_dev, cycle_size, tok_dev, head_dev)...  8.11 us
    dynamic_slice x8, local copies, waits for them, and re-layouts, shards(): lax.map(one_block, (blocks, jnp.arange(block_total, dtype=jnp.int32)))  4.94 us
  transfers between devices with their start and end apart: 2, of which 2 were waited for; matrix products, arithmetic and copies ran while one was open for 1% of the time, Pallas kernels for 0%

commit v1 on v0

--- a/solution.py
+++ b/solution.py
@@ -14,7 +14,12 @@
     cycle_size = lax.axis_size("ctx")
     score_scale = 1.0 / head_dim**0.5
     key_position = lax.axis_index("ctx") * ctx_dev + jnp.arange(ctx_dev, dtype=jnp.int32)
-    piece_rows = lax.all_gather(queries, "ctx", axis=1, tiled=True)
+    ring = [queries]
+    for hop in range(3):
+        ring.append(lax.ppermute(ring[-1], "ctx", [(dev, (dev + 1) % 4) for dev in range(4)]))
+    piece_rows = jnp.roll(
+        jnp.concatenate(ring[::-1], axis=1), (lax.axis_index("ctx") + 1) * ring[0].shape[1], axis=1
+    )
     row_count = piece_rows.shape[1]
     block_size = 64
     block_total = row_count // block_size

time: 184 us -> 162 us (0.88)
  between operations: 13.5 us -> 0.16 us
  waiting for transfers between devices: 95.4 us -> 85.6 us
  matrix products: 27.3 us -> 19.7 us
  local copies, waits for them, and re-layouts: 8.89 us -> 15.3 us
  starting transfers between devices: 3.61 us -> 6.66 us
    all_gather x1 -> x0, waiting for transfers between devices: 47.8 us -> none  [shards(): piece_rows = lax.all_gather(queries, 'ctx', axis=1, tiled=True)]
    ppermute x0 -> x3, waiting for transfers between devices: none -> 40.9 us  [shards(): lax.ppermute(ring[-1], 'ctx', [(dev, (dev + 1) % 4) for dev in range(4)])]
    dot_general x8, matrix products: 16.8 us -> 9.16 us  [one_block(): jnp.einsum('cbkgd,cskd->ckbgs', query_block, keys, preferred_element_type...]
    dynamic_update_slice x16, local copies, waits for them, and re-layouts: 0.9 us -> 6.41 us  [shards(): lax.map(one_block, (blocks, jnp.arange(block_total, dtype=jnp.int32)))]
    ppermute x0 -> x3, starting transfers between devices: none -> 3.06 us  [shards(): lax.ppermute(ring[-1], 'ctx', [(dev, (dev + 1) % 4) for dev in range(4)])]
    all_to_all x1, waiting for transfers between devices: 46.9 us -> 44.7 us  [shards(): lax.all_to_all(partial_value.reshape(conv_dev, cycle_size, tok_dev, head_...]
  transfers between devices with their start and end apart: 2 -> 4, of which waited for: 2 -> 4; matrix products, arithmetic and copies ran while one was open for 1% -> 2% of each run, Pallas kernels for 0% -> 0%
where the time goes in v1:
time: 162 us
  waiting for transfers between devices  85.6 us (53%)
  matrix products  19.7 us (12%)
  other arithmetic  15.5 us (10%)
  local copies, waits for them, and re-layouts  15.3 us (9%)
  loops' own time  10.6 us (7%)
  blocking collectives  8.01 us (5%)
  starting transfers between devices  6.66 us (4%)
    all_to_all x1, waiting for transfers between devices, shards(): lax.all_to_all(partial_value.reshape(conv_dev, cycle_size, tok_dev, head_...  44.7 us
    ppermute x3, waiting for transfers between devices, shards(): lax.ppermute(ring[-1], 'ctx', [(dev, (dev + 1) % 4) for dev in range(4)])  40.9 us
    reduce_sum x8, other arithmetic, one_block(): exp_total = jnp.sum(weights, axis=-1)  11.8 us
    another operation x1, loops' own time, shards(): lax.map(one_block, (blocks, jnp.arange(block_total, dtype=jnp.int32)))  10.6 us
    dot_general x8, matrix products, one_block(): jnp.einsum('ckbgs,cskd->ckbgd', rounded, values, preferred_element_type=j...  10.5 us
    dot_general x8, matrix products, one_block(): jnp.einsum('cbkgd,cskd->ckbgs', query_block, keys, preferred_element_type...  9.16 us
    all_to_all x1, blocking collectives, shards(): lax.all_to_all(log_total.reshape(conv_dev, cycle_size, tok_dev, head_dev)...  8.01 us
    dynamic_update_slice x16, local copies, waits for them, and re-layouts, shards(): lax.map(one_block, (blocks, jnp.arange(block_total, dtype=jnp.int32)))  6.41 us
  transfers between devices with their start and end apart: 4, of which 4 were waited for; matrix products, arithmetic and copies ran while one was open for 2% of the time, Pallas kernels for 0%

profile of v1, /device:TPU:0, one launch (start us, length us, event | category | flops | bytes accessed | tf_op | source)
XLA Modules:
  0.0 161.6 jit_solution(10022397274347340649)
XLA Ops:
  0.0 3.1 %collective-permute-start = (bf16[1,128,16,128]{3,2,1,0:T(8,128)(2,1)}, bf16[1,128,16,128]{3,2,1,0:T(8,128)(2,1)S(1)}, u32[]{:S(2)}, u32[]{:S(2)}) collective-permute-start(bf16[1,128,16,128]{3,2,1,0:T(8,128)(2,1)} %param.6), channel_id=1, source_target_pairs={{0,8},{8,16},{16,24},{24,0},{1,9},{9,17},{17,25},{25,1},{2,10},{10... | collective-permute-start | bytes 1572872 | tf_op jit(solution)/shard_map/ppermute | solution.py:19
  3.1 14.2 %collective-permute-done = bf16[1,128,16,128]{3,2,1,0:T(8,128)(2,1)S(1)} collective-permute-done((bf16[1,128,16,128]{3,2,1,0:T(8,128)(2,1)}, bf16[1,128,16,128]{3,2,1,0:T(8,128)(2,1)S(1)}, u32[]{:S(2)}, u32[]{:S(2)}) %collective-permute-start) | collective-permute-done | bytes 524320 | tf_op jit(solution)/shard_map/ppermute | solution.py:19
  17.3 14.9 %collective-permute-done.1 = bf16[1,128,16,128]{3,2,1,0:T(8,128)(2,1)S(1)} collective-permute-done((bf16[1,128,16,128]{3,2,1,0:T(8,128)(2,1)S(1)}, bf16[1,128,16,128]{3,2,1,0:T(8,128)(2,1)S(1)}, u32[]{:S(2)}, u32[]{:S(2)}) %collective-permute-start.1) | collective-permute-done | bytes 524320 | tf_op jit(solution)/shard_map/ppermute | solution.py:19
  34.4 11.8 %collective-permute-done.2 = bf16[1,128,16,128]{3,2,1,0:T(8,128)(2,1)S(1)} collective-permute-done((bf16[1,128,16,128]{3,2,1,0:T(8,128)(2,1)S(1)}, bf16[1,128,16,128]{3,2,1,0:T(8,128)(2,1)S(1)}, u32[]{:S(2)}, u32[]{:S(2)}) %collective-permute-start.2) | collective-permute-done | bytes 524320 | tf_op jit(solution)/shard_map/ppermute | solution.py:19
  47.2 54.9 %while.13 = (s32[]{:T(128)}, bf16[8,1,64,16,128]{4,3,2,1,0:T(8,128)(2,1)}, f32[8,1,64,16]{2,0,3,1:T(8,128)S(1)}, s32[8]{0:T(128)S(1)}, s32[1]{0:T(128)}, /*index...) while((s32[]{:T(128)}, ...), condition=%wide.region_3.4_spmd.clone, body=%wide.region_0.3_spmd.clone.sunk | while | flops 550831168 | bytes 15004841 | solution.py:60
  49.2 1.1 fusion.34
  50.4 1.5 fusion.35
  51.9 1.3 fusion.36
  56.1 1.1 fusion.34
  57.2 1.5 fusion.35
  58.7 1.3 fusion.36
  62.9 1.1 fusion.34
  64.1 1.5 fusion.35
  65.6 1.3 fusion.36
  69.8 1.1 fusion.34
  70.9 1.5 fusion.35
  72.4 1.3 fusion.36
  76.7 1.1 fusion.34
  77.8 1.5 fusion.35
  79.3 1.3 fusion.36
  83.5 1.1 fusion.34
  84.7 1.5 fusion.35
  86.2 1.3 fusion.36
  90.4 1.1 fusion.34
  91.6 1.5 fusion.35
  93.1 1.3 fusion.36
  98.4 1.5 fusion.35
  99.9 1.3 fusion.36
  102.2 8.0 %all_to_all.10 = f32[1,4,128,16]{2,3,0,1:T(8,128)S(1)} all-to-all(f32[1,4,128,16]{2,3,0,1:T(8,128)S(1)} %copy.21), channel_id=1, replica_groups=mesh['ctx'=4,'kvh'=4,'conv'=2] {'ctx'}, dimensions={1} | all-to-all | bytes 65536 | tf_op jit(solution)/shard_map/all_to_all | solution.py:75
  110.2 3.6 %all-to-all-start.1 = ((bf16[1,4,128,16,128]{4,3,2,0,1:T(8,128)(2,1)}), bf16[1,4,128,16,128]{4,3,2,0,1:T(8,128)(2,1)S(1)}, u32[]{:S(2)}, u32[]{:S(2)}) async-start(bf16[1,4,128,16,128]{4,3,2,0,1:T(8,128)(2,1)} %bitcast.61), calls=%async_computation.1 | async-start | bytes 4194304 | tf_op jit(solution)/shard_map/all_to_all | solution.py:68
  114.1 44.7 %all-to-all-done.1 = bf16[1,4,128,16,128]{4,3,2,0,1:T(8,128)(2,1)S(1)} async-done(((bf16[1,4,128,16,128]{4,3,2,0,1:T(8,128)(2,1)}), bf16[1,4,128,16,128]{4,3,2,0,1:T(8,128)(2,1)S(1)}, u32[]{:S(2)}, u32[]{:S(2)}) %all-to-all-start.1) | async-done | bytes 2097184 | tf_op jit(solution)/shard_map/all_to_all | solution.py:68
  158.9 1.5 multiply_reduce_fusion
  (90 shorter events, 18.7 us)
Async XLA Ops:
  0.0 46.4 %copy-start = (bf16[1,128,16,128]{3,2,1,0:T(8,128)(2,1)S(1)}, bf16[1,128,16,128]{3,2,1,0:T(8,128)(2,1)}, u32[]{:S(2)}) copy-start(bf16[1,128,16,128]{3,2,1,0:T(8,128)(2,1)} %param.6) | copy-start | bytes 1572868
  0.0 17.3 %collective-permute-start = (bf16[1,128,16,128]{3,2,1,0:T(8,128)(2,1)}, bf16[1,128,16,128]{3,2,1,0:T(8,128)(2,1)S(1)}, u32[]{:S(2)}, u32[]{:S(2)}) collective-permute-start(bf16[1,128,16,128]{3,2,1,0:T(8,128)(2,1)} %param.6), channel_id=1, source_target_pairs={{0,8},{8,16},{16,24},{24,0},{1,9},{9,17},{17,25},{25,1},{2,10},{10... | collective-permute-start | bytes 1572872 | tf_op jit(solution)/shard_map/ppermute | solution.py:19
  17.3 14.9 %collective-permute-start.1 = (bf16[1,128,16,128]{3,2,1,0:T(8,128)(2,1)S(1)}, bf16[1,128,16,128]{3,2,1,0:T(8,128)(2,1)S(1)}, u32[]{:S(2)}, u32[]{:S(2)}) collective-permute-start(bf16[1,128,16,128]{3,2,1,0:T(8,128)(2,1)S(1)} %collective-permute-done), channel_id=1, source_target_pairs={{0,8},{8,16},{16,24},{24,0},{1,9},{9,17},{17,25},{25,1},{2,10},{10... | collective-permute-start | bytes 1572872 | tf_op jit(solution)/shard_map/ppermute | solution.py:19
  32.2 14.0 %collective-permute-start.2 = (bf16[1,128,16,128]{3,2,1,0:T(8,128)(2,1)S(1)}, bf16[1,128,16,128]{3,2,1,0:T(8,128)(2,1)S(1)}, u32[]{:S(2)}, u32[]{:S(2)}) collective-permute-start(bf16[1,128,16,128]{3,2,1,0:T(8,128)(2,1)S(1)} %collective-permute-done.1), channel_id=1, source_target_pairs={{0,8},{8,16},{16,24},{24,0},{1,9},{9,17},{17,25},{25,1},{2,10},{10... | collective-permute-start | bytes 1572872 | tf_op jit(solution)/shard_map/ppermute | solution.py:19
  110.2 48.6 %all-to-all-start.1 = ((bf16[1,4,128,16,128]{4,3,2,0,1:T(8,128)(2,1)}), bf16[1,4,128,16,128]{4,3,2,0,1:T(8,128)(2,1)S(1)}, u32[]{:S(2)}, u32[]{:S(2)}) async-start(bf16[1,4,128,16,128]{4,3,2,0,1:T(8,128)(2,1)} %bitcast.61), calls=%async_computation.1 | async-start | bytes 4194304 | tf_op jit(solution)/shard_map/all_to_all | solution.py:68
